TPU v7x, 32 devices: a whole 2x2x4 slice. The times are simulated.
32 devices in a mesh: ma: 8 (over z, x), band: 4 (over y, core).
Axes of the slice: x: 2, y: 2, z: 4, core: 2. Of those that a mesh axis runs over, the one named last changes fastest.
Arguments:
- observed: bfloat16 [256, 64, 1024], P(('ma', 'band')), may hold values from -6 to 6
- eigenvalues: float32 [256, 1024], P(('ma', 'band')), may hold values from 0.05 to 20
- kl_basis: bfloat16 [256, 1024, 512], P(('ma', 'band')), may hold values from -0.1875 to 0.1875
- band_deriv: bfloat16 [40, 512, 512], P('band'), may hold values from -0.15625 to 0.15625, as said below
- counts: int32 [256], P(('ma', 'band')), may hold values from 128 to 1024, as said below
Outputs:
- mode_power: float32 [256, 40], P('ma', 'band')
- band_power: float32 [40], P('band')
Inputs may be any that keep to these rules, and one draw needn't show every extreme that they name: counts[m] is the number of leading KL modes of m-mode m that are kept; some m-mode keeps 1024 and some keeps 1024 // 8. Each band_deriv[a] is symmetric.
All inputs are finite; a program needn't handle non-finite values.
Results may differ from a plain program's by a relative error of at most 0.0018.
Values may be sent and summed in bfloat16 or wider, within the bound.
No kernel may reach another device: no remote copies, remote signals or barrier semaphores. Data moves between devices by JAX's collectives and lax.ppermute only.
A program may use at most 64 MiB of HBM per device.

v0:
```python
import jax
import jax.numpy as jnp
from jax import lax
from jax.sharding import PartitionSpec as P


def weigh(observed, eigenvalues, counts):
    position = lax.broadcasted_iota(jnp.int32, eigenvalues.shape, 1)
    inside = position < counts[:, None]
    weights = jnp.where(inside, 1.0 / (1.0 + eigenvalues), jnp.zeros_like(eigenvalues))
    return (observed.astype(jnp.float32) * weights[:, None, :]).astype(jnp.bfloat16)


def project_padded(weighted, kl_basis):
    return jnp.einsum("msi,miw->msw", weighted, kl_basis, preferred_element_type=jnp.float32)


def band_quadratic(vectors, matrices):
    mode_count = vectors.shape[0]
    flattened = vectors.reshape(mode_count * vectors.shape[1], vectors.shape[2])

    def one_band(matrix):
        mapped = jnp.dot(flattened, matrix, preferred_element_type=jnp.float32)
        return jnp.sum((mapped * flattened).reshape(mode_count, -1), axis=1)

    return lax.map(one_band, matrices)


def per_device(observed, eigenvalues, kl_basis, band_deriv, counts):
    samples = observed.shape[1]
    live_total = lax.psum(jnp.sum(counts).astype(jnp.float32), ("ma", "band"))
    weighted = weigh(observed, eigenvalues, counts)
    projected = project_padded(weighted, kl_basis)
    projected = projected.astype(jnp.bfloat16)
    quadratic = band_quadratic(lax.all_gather(projected, "band", axis=0, tiled=True), band_deriv)
    mode_power = jnp.transpose(quadratic) / samples
    partial_sum = jnp.sum(mode_power, axis=0)
    band_total = lax.psum(partial_sum, "ma")
    band_power = observed.shape[2] * band_total / live_total
    return (mode_power, band_power)


def solution(mesh):
    in_specs = (
        P(("ma", "band"), None, None),
        P(("ma", "band"), None),
        P(("ma", "band"), None, None),
        P("band", None, None),
        P(("ma", "band")),
    )
    out_specs = (P("ma", "band"), P("band"))
    return jax.shard_map(
        per_device, mesh=mesh, in_specs=in_specs, out_specs=out_specs, check_vma=False
    )
```

profile of v0, /device:TPU:0, one launch (start us, length us, event | category | flops | bytes accessed | tf_op | source)
XLA Modules:
  0.0 117.1 jit_solution(10019816696674286477)
XLA Ops:
  7.2 0.8 divide_select_fusion
  8.0 6.0 %convolution_convert_fusion = bf16[8,64,512]{2,1,0:T(8,128)(2,1)} fusion(bf16[8,1024,512]{2,1,0:T(8,128)(2,1)} %param.9, bf16[8,64,1024]{2,1,0:T(8,128)(2,1)} %param.7, f32[8,1024]{1,0:T(8,128)S(1)} %divide_select_fusion), kind=kOutput, calls=%fused_computation.6 | convolution fusion | flops 538705920 | bytes 9994240 | tf_op jit(solution)/shard_map/msi,miw->msw/dot_general | solution.py:15
  14.1 0.6 reduce_sum.35
  15.4 42.4 %psum.15 = f32[]{:T(128)} all-reduce(f32[]{:T(128)S(6)} %convert_element_type.18), channel_id=1, replica_groups=mesh['ma'=8,'band'=4] {'ma','band'}, use_global_device_ids=true, to_apply=%region_7.8 | all-reduce | flops 1 | bytes 8 | tf_op jit(solution)/shard_map/psum | solution.py:31
  57.8 2.9 %copy.9 = bf16[2048,512]{0,1:T(8,128)(2,1)S(1)} copy(bf16[2048,512]{1,0:T(8,128)(2,1)} %bitcast.21) | data formatting | bytes 4194304 | tf_op jit(solution)/shard_map/while | solution.py:26
  60.8 26.6 %while.10 = (s32[]{:T(128)}, f32[10,32]{1,0:T(8,128)S(1)}, bf16[10,512,512]{2,1,0:T(8,128)(2,1)}, bf16[2048,512]{0,1:T(8,128)(2,1)S(1)}, s32[]{:T(128)}, /*index=5*/f32[]{:T(128)}, s32[]{:T(128)}) while((s32[]{:T(128)}, f32[10,32]{1,0:T(8,128)S(1)}, bf16[10,512,512]{2,1,0:T(8,128)(2,1)}, bf16[2048,512]{0,1:T(8,128)(2,1)S(1)}, s32[]{:T(128)}, ...), condition=%wide.region_3.4_spmd, body=%wide.region_0.3_spmd.sunk | while | flops 1076887552 | bytes 4752341 | solution.py:26
  60.8 2.4 %fusion.12 = f32[2048]{0:T(1024)S(1)} fusion(bf16[2048,512]{0,1:T(8,128)(2,1)S(1)} %get-tuple-element.89, bf16[10,512,512]{2,1,0:T(8,128)(2,1)} %get-tuple-element.88, s32[]{:T(128)} %get-tuple-element.79), kind=kOutput, calls=%fused_computation.1.clone.1 | convolution fusion | flops 1076885504 | bytes 4727296 | tf_op jit(solution)/shard_map/while/body/eval_jaxpr/dot_general | solution.py:23
  63.3 0.1 reduce_sum.43
  63.4 2.4 %fusion.12 = f32[2048]{0:T(1024)S(1)} fusion(bf16[2048,512]{0,1:T(8,128)(2,1)S(1)} %get-tuple-element.89, bf16[10,512,512]{2,1,0:T(8,128)(2,1)} %get-tuple-element.88, s32[]{:T(128)} %get-tuple-element.79), kind=kOutput, calls=%fused_computation.1.clone.1 | convolution fusion | flops 1076885504 | bytes 4727296 | tf_op jit(solution)/shard_map/while/body/eval_jaxpr/dot_general | solution.py:23
  65.9 0.1 reduce_sum.43
  66.1 2.4 %fusion.12 = f32[2048]{0:T(1024)S(1)} fusion(bf16[2048,512]{0,1:T(8,128)(2,1)S(1)} %get-tuple-element.89, bf16[10,512,512]{2,1,0:T(8,128)(2,1)} %get-tuple-element.88, s32[]{:T(128)} %get-tuple-element.79), kind=kOutput, calls=%fused_computation.1.clone.1 | convolution fusion | flops 1076885504 | bytes 4727296 | tf_op jit(solution)/shard_map/while/body/eval_jaxpr/dot_general | solution.py:23
  68.6 0.1 reduce_sum.43
  68.7 2.4 %fusion.12 = f32[2048]{0:T(1024)S(1)} fusion(bf16[2048,512]{0,1:T(8,128)(2,1)S(1)} %get-tuple-element.89, bf16[10,512,512]{2,1,0:T(8,128)(2,1)} %get-tuple-element.88, s32[]{:T(128)} %get-tuple-element.79), kind=kOutput, calls=%fused_computation.1.clone.1 | convolution fusion | flops 1076885504 | bytes 4727296 | tf_op jit(solution)/shard_map/while/body/eval_jaxpr/dot_general | solution.py:23
  71.2 0.1 reduce_sum.43
  71.4 2.4 %fusion.12 = f32[2048]{0:T(1024)S(1)} fusion(bf16[2048,512]{0,1:T(8,128)(2,1)S(1)} %get-tuple-element.89, bf16[10,512,512]{2,1,0:T(8,128)(2,1)} %get-tuple-element.88, s32[]{:T(128)} %get-tuple-element.79), kind=kOutput, calls=%fused_computation.1.clone.1 | convolution fusion | flops 1076885504 | bytes 4727296 | tf_op jit(solution)/shard_map/while/body/eval_jaxpr/dot_general | solution.py:23
  73.9 0.1 reduce_sum.43
  74.1 2.4 %fusion.12 = f32[2048]{0:T(1024)S(1)} fusion(bf16[2048,512]{0,1:T(8,128)(2,1)S(1)} %get-tuple-element.89, bf16[10,512,512]{2,1,0:T(8,128)(2,1)} %get-tuple-element.88, s32[]{:T(128)} %get-tuple-element.79), kind=kOutput, calls=%fused_computation.1.clone.1 | convolution fusion | flops 1076885504 | bytes 4727296 | tf_op jit(solution)/shard_map/while/body/eval_jaxpr/dot_general | solution.py:23
  76.7 2.4 %fusion.12 = f32[2048]{0:T(1024)S(1)} fusion(bf16[2048,512]{0,1:T(8,128)(2,1)S(1)} %get-tuple-element.89, bf16[10,512,512]{2,1,0:T(8,128)(2,1)} %get-tuple-element.88, s32[]{:T(128)} %get-tuple-element.79), kind=kOutput, calls=%fused_computation.1.clone.1 | convolution fusion | flops 1076885504 | bytes 4727296 | tf_op jit(solution)/shard_map/while/body/eval_jaxpr/dot_general | solution.py:23
  79.4 2.4 %fusion.12 = f32[2048]{0:T(1024)S(1)} fusion(bf16[2048,512]{0,1:T(8,128)(2,1)S(1)} %get-tuple-element.89, bf16[10,512,512]{2,1,0:T(8,128)(2,1)} %get-tuple-element.88, s32[]{:T(128)} %get-tuple-element.79), kind=kOutput, calls=%fused_computation.1.clone.1 | convolution fusion | flops 1076885504 | bytes 4727296 | tf_op jit(solution)/shard_map/while/body/eval_jaxpr/dot_general | solution.py:23
  82.0 2.4 %fusion.12 = f32[2048]{0:T(1024)S(1)} fusion(bf16[2048,512]{0,1:T(8,128)(2,1)S(1)} %get-tuple-element.89, bf16[10,512,512]{2,1,0:T(8,128)(2,1)} %get-tuple-element.88, s32[]{:T(128)} %get-tuple-element.79), kind=kOutput, calls=%fused_computation.1.clone.1 | convolution fusion | flops 1076885504 | bytes 4727296 | tf_op jit(solution)/shard_map/while/body/eval_jaxpr/dot_general | solution.py:23
  84.7 2.4 %fusion.12 = f32[2048]{0:T(1024)S(1)} fusion(bf16[2048,512]{0,1:T(8,128)(2,1)S(1)} %get-tuple-element.89, bf16[10,512,512]{2,1,0:T(8,128)(2,1)} %get-tuple-element.88, s32[]{:T(128)} %get-tuple-element.79), kind=kOutput, calls=%fused_computation.1.clone.1 | convolution fusion | flops 1076885504 | bytes 4727296 | tf_op jit(solution)/shard_map/while/body/eval_jaxpr/dot_general | solution.py:23
  87.3 0.7 multiply_reduce_fusion
  88.0 21.1 %psum.14 = f32[10]{0:T(128)S(1)} all-reduce(f32[10]{0:T(128)S(1)} %get-tuple-element.45), channel_id=1, replica_groups=mesh['ma'=8,'band'=4] {'ma'}, use_global_device_ids=true, to_apply=%region_5.6 | all-reduce | flops 10 | bytes 80 | tf_op jit(solution)/shard_map/psum | solution.py:38
  109.1 1.1 multiply_divide_fusion
  (31 shorter events, 1.7 us)
Async XLA Ops:
  7.2 50.7 %all-gather.2.cloned.1.call-start = ((), (), s32[]{:S(2)}) async-start(), calls=%async_computation | async-start | bytes 2621440 | tf_op jit(solution)/shard_map/all_gather | solution.py:35
  8.0 6.1 %copy-start = (s32[8]{0:T(128)S(1)}, s32[8]{0:T(128)}, u32[]{:S(2)}) copy-start(s32[8]{0:T(128)} %param.11) | copy-start | bytes 100
Sparse Core Ops, SparseCore 0:
  14.2 25.4 all-gather.1
where the time goes:
time: 118 us; the launch traced here: 117 us
  blocking collectives  63.5 us (54%)
  matrix products  30.2 us (26%)
  between operations  14.7 us (12%)
  other arithmetic  4.47 us (4%)
  local copies, waits for them, and re-layouts  3.98 us (3%)
    psum x1, blocking collectives, per_device(): live_total = lax.psum(jnp.sum(counts).astype(jnp.float32), ('ma', 'band'))  42.4 us
    dot_general x10, matrix products, one_band(): mapped = jnp.dot(flattened, matrix, preferred_element_type=jnp.float32)  24.1 us
    psum x1, blocking collectives, per_device(): band_total = lax.psum(partial_sum, 'ma')  21.1 us
    dot_general x1, matrix products, project_padded(): jnp.einsum('msi,miw->msw', weighted, kl_basis, preferred_element_type=jnp...  6.04 us
    while x1, local copies, waits for them, and re-layouts, band_quadratic(): return lax.map(one_band, matrices)  2.93 us
  transfers between devices with their start and end apart: 1, of which 0 were waited for; matrix products, arithmetic and copies ran while one was open for 1% of the time, Pallas kernels for 0%

commit v1 on v0

--- a/solution.py
+++ b/solution.py
@@ -2,6 +2,11 @@
 import jax.numpy as jnp
 from jax import lax
 from jax.sharding import PartitionSpec as P
+
+
+def gather_and_add(array, axis):
+    terms = lax.all_gather(array, axis)
+    return jnp.sum(terms, axis=0)
 
 
 def weigh(observed, eigenvalues, counts):
@@ -28,7 +33,7 @@
 
 def per_device(observed, eigenvalues, kl_basis, band_deriv, counts):
     samples = observed.shape[1]
-    live_total = lax.psum(jnp.sum(counts).astype(jnp.float32), ("ma", "band"))
+    live_total = gather_and_add(jnp.sum(counts).astype(jnp.float32), ("ma", "band"))
     weighted = weigh(observed, eigenvalues, counts)
     projected = project_padded(weighted, kl_basis)
     projected = projected.astype(jnp.bfloat16)

time: 118 us -> 118 us (level)
    psum x1 -> x0, blocking collectives: 42.4 us -> none  [per_device(): live_total = lax.psum(jnp.sum(counts).astype(jnp.float32), ('ma', 'band'))]
    unnamed x0 -> x1, blocking collectives: none -> 42.2 us
where the time goes in v1:
time: 118 us
  blocking collectives  63.3 us (54%)
  matrix products  30.1 us (26%)
  between operations  14.7 us (12%)
  other arithmetic  5.07 us (4%)
  local copies, waits for them, and re-layouts  4.1 us (3%)
    unnamed x1, blocking collectives  42.2 us
    dot_general x10, matrix products, one_band(): mapped = jnp.dot(flattened, matrix, preferred_element_type=jnp.float32)  24.1 us
    psum x1, blocking collectives, per_device(): band_total = lax.psum(partial_sum, 'ma')  21.1 us
    dot_general x1, matrix products, project_padded(): jnp.einsum('msi,miw->msw', weighted, kl_basis, preferred_element_type=jnp...  6.04 us
    while x1, local copies, waits for them, and re-layouts, band_quadratic(): return lax.map(one_band, matrices)  2.92 us
  transfers between devices with their start and end apart: 1, of which 0 were waited for; matrix products, arithmetic and copies ran while one was open for 1% of the time, Pallas kernels for 0%

profile of v1, /device:TPU:0, one launch (start us, length us, event | category | flops | bytes accessed | tf_op | source)
XLA Modules:
  0.0 117.7 jit_solution(12229999035581839562)
XLA Ops:
  7.2 0.8 divide_select_fusion
  8.0 6.0 %convolution_convert_fusion = bf16[8,64,512]{2,1,0:T(8,128)(2,1)} fusion(bf16[8,1024,512]{2,1,0:T(8,128)(2,1)} %param.9, bf16[8,64,1024]{2,1,0:T(8,128)(2,1)} %param.7, f32[8,1024]{1,0:T(8,128)S(1)} %divide_select_fusion), kind=kOutput, calls=%fused_computation.6 | convolution fusion | flops 538705920 | bytes 9994240 | tf_op jit(solution)/shard_map/msi,miw->msw/dot_general | solution.py:20
  14.1 0.6 reduce_sum.44
  15.5 42.2 %all-reduce = f32[32]{0:T(128)S(1)} all-reduce(f32[32]{0:T(128)S(1)} %dynamic-update-slice), channel_id=1, replica_groups=mesh['ma'=8,'band'=4] {'ma','band'}, use_global_device_ids=true, to_apply=%add | all-reduce | flops 32 | bytes 256
  57.8 0.6 reduce_sum.45
  58.4 2.9 %copy.9 = bf16[2048,512]{0,1:T(8,128)(2,1)S(1)} copy(bf16[2048,512]{1,0:T(8,128)(2,1)} %bitcast.22) | data formatting | bytes 4194304 | tf_op jit(solution)/shard_map/while | solution.py:31
  61.3 26.5 %while.10 = (s32[]{:T(128)}, f32[10,32]{1,0:T(8,128)S(1)}, bf16[10,512,512]{2,1,0:T(8,128)(2,1)}, bf16[2048,512]{0,1:T(8,128)(2,1)S(1)}, s32[]{:T(128)}, /*index=5*/f32[]{:T(128)}, s32[]{:T(128)}) while((s32[]{:T(128)}, f32[10,32]{1,0:T(8,128)S(1)}, bf16[10,512,512]{2,1,0:T(8,128)(2,1)}, bf16[2048,512]{0,1:T(8,128)(2,1)S(1)}, s32[]{:T(128)}, ...), condition=%wide.region_3.4_spmd, body=%wide.region_0.3_spmd.sunk | while | flops 1076887552 | bytes 4752341 | solution.py:31
  61.3 2.4 %fusion.12 = f32[2048]{0:T(1024)S(1)} fusion(bf16[2048,512]{0,1:T(8,128)(2,1)S(1)} %get-tuple-element.89, bf16[10,512,512]{2,1,0:T(8,128)(2,1)} %get-tuple-element.88, s32[]{:T(128)} %get-tuple-element.79), kind=kOutput, calls=%fused_computation.1.clone.1 | convolution fusion | flops 1076885504 | bytes 4727296 | tf_op jit(solution)/shard_map/while/body/eval_jaxpr/dot_general | solution.py:28
  64.0 2.4 %fusion.12 = f32[2048]{0:T(1024)S(1)} fusion(bf16[2048,512]{0,1:T(8,128)(2,1)S(1)} %get-tuple-element.89, bf16[10,512,512]{2,1,0:T(8,128)(2,1)} %get-tuple-element.88, s32[]{:T(128)} %get-tuple-element.79), kind=kOutput, calls=%fused_computation.1.clone.1 | convolution fusion | flops 1076885504 | bytes 4727296 | tf_op jit(solution)/shard_map/while/body/eval_jaxpr/dot_general | solution.py:28
  66.6 2.4 %fusion.12 = f32[2048]{0:T(1024)S(1)} fusion(bf16[2048,512]{0,1:T(8,128)(2,1)S(1)} %get-tuple-element.89, bf16[10,512,512]{2,1,0:T(8,128)(2,1)} %get-tuple-element.88, s32[]{:T(128)} %get-tuple-element.79), kind=kOutput, calls=%fused_computation.1.clone.1 | convolution fusion | flops 1076885504 | bytes 4727296 | tf_op jit(solution)/shard_map/while/body/eval_jaxpr/dot_general | solution.py:28
  69.1 0.1 reduce_sum.53
  69.3 2.4 %fusion.12 = f32[2048]{0:T(1024)S(1)} fusion(bf16[2048,512]{0,1:T(8,128)(2,1)S(1)} %get-tuple-element.89, bf16[10,512,512]{2,1,0:T(8,128)(2,1)} %get-tuple-element.88, s32[]{:T(128)} %get-tuple-element.79), kind=kOutput, calls=%fused_computation.1.clone.1 | convolution fusion | flops 1076885504 | bytes 4727296 | tf_op jit(solution)/shard_map/while/body/eval_jaxpr/dot_general | solution.py:28
  71.9 2.4 %fusion.12 = f32[2048]{0:T(1024)S(1)} fusion(bf16[2048,512]{0,1:T(8,128)(2,1)S(1)} %get-tuple-element.89, bf16[10,512,512]{2,1,0:T(8,128)(2,1)} %get-tuple-element.88, s32[]{:T(128)} %get-tuple-element.79), kind=kOutput, calls=%fused_computation.1.clone.1 | convolution fusion | flops 1076885504 | bytes 4727296 | tf_op jit(solution)/shard_map/while/body/eval_jaxpr/dot_general | solution.py:28
  74.4 0.1 reduce_sum.53
  74.6 2.4 %fusion.12 = f32[2048]{0:T(1024)S(1)} fusion(bf16[2048,512]{0,1:T(8,128)(2,1)S(1)} %get-tuple-element.89, bf16[10,512,512]{2,1,0:T(8,128)(2,1)} %get-tuple-element.88, s32[]{:T(128)} %get-tuple-element.79), kind=kOutput, calls=%fused_computation.1.clone.1 | convolution fusion | flops 1076885504 | bytes 4727296 | tf_op jit(solution)/shard_map/while/body/eval_jaxpr/dot_general | solution.py:28
  77.3 2.4 %fusion.12 = f32[2048]{0:T(1024)S(1)} fusion(bf16[2048,512]{0,1:T(8,128)(2,1)S(1)} %get-tuple-element.89, bf16[10,512,512]{2,1,0:T(8,128)(2,1)} %get-tuple-element.88, s32[]{:T(128)} %get-tuple-element.79), kind=kOutput, calls=%fused_computation.1.clone.1 | convolution fusion | flops 1076885504 | bytes 4727296 | tf_op jit(solution)/shard_map/while/body/eval_jaxpr/dot_general | solution.py:28
  79.7 0.1 reduce_sum.53
  79.9 2.4 %fusion.12 = f32[2048]{0:T(1024)S(1)} fusion(bf16[2048,512]{0,1:T(8,128)(2,1)S(1)} %get-tuple-element.89, bf16[10,512,512]{2,1,0:T(8,128)(2,1)} %get-tuple-element.88, s32[]{:T(128)} %get-tuple-element.79), kind=kOutput, calls=%fused_computation.1.clone.1 | convolution fusion | flops 1076885504 | bytes 4727296 | tf_op jit(solution)/shard_map/while/body/eval_jaxpr/dot_general | solution.py:28
  82.6 2.4 %fusion.12 = f32[2048]{0:T(1024)S(1)} fusion(bf16[2048,512]{0,1:T(8,128)(2,1)S(1)} %get-tuple-element.89, bf16[10,512,512]{2,1,0:T(8,128)(2,1)} %get-tuple-element.88, s32[]{:T(128)} %get-tuple-element.79), kind=kOutput, calls=%fused_computation.1.clone.1 | convolution fusion | flops 1076885504 | bytes 4727296 | tf_op jit(solution)/shard_map/while/body/eval_jaxpr/dot_general | solution.py:28
  85.2 2.4 %fusion.12 = f32[2048]{0:T(1024)S(1)} fusion(bf16[2048,512]{0,1:T(8,128)(2,1)S(1)} %get-tuple-element.89, bf16[10,512,512]{2,1,0:T(8,128)(2,1)} %get-tuple-element.88, s32[]{:T(128)} %get-tuple-element.79), kind=kOutput, calls=%fused_computation.1.clone.1 | convolution fusion | flops 1076885504 | bytes 4727296 | tf_op jit(solution)/shard_map/while/body/eval_jaxpr/dot_general | solution.py:28
  87.7 0.1 reduce_sum.53
  87.9 0.7 multiply_reduce_fusion
  88.6 21.1 %psum.7 = f32[10]{0:T(128)S(1)} all-reduce(f32[10]{0:T(128)S(1)} %get-tuple-element.45), channel_id=1, replica_groups=mesh['ma'=8,'band'=4] {'ma'}, use_global_device_ids=true, to_apply=%region_5.6 | all-reduce | flops 10 | bytes 80 | tf_op jit(solution)/shard_map/psum | solution.py:43
  109.7 1.1 multiply_divide_fusion
  (34 shorter events, 1.9 us)
Async XLA Ops:
  7.2 51.2 %all-gather.2.cloned.1.call-start = ((), (), s32[]{:S(2)}) async-start(), calls=%async_computation | async-start | bytes 2621440 | tf_op jit(solution)/shard_map/all_gather | solution.py:40
  8.0 6.1 %copy-start = (s32[8]{0:T(128)S(1)}, s32[8]{0:T(128)}, u32[]{:S(2)}) copy-start(s32[8]{0:T(128)} %param.11) | copy-start | bytes 100
Sparse Core Ops, SparseCore 0:
  14.2 25.4 all-gather.1
